TPU v7x, 128 devices: a whole 4x4x4 slice. The times are simulated.
128 devices in a mesh: tm: 16 (over z, x), pair: 8 (over y, core).
Axes of the slice: x: 4, y: 4, z: 4, core: 2. Of those that a mesh axis runs over, the one named last changes fastest.
Arguments:
- signal: float32 [2, 262144], P(None, 'tm'), may hold values from -6 to 6
- hop_offsets: int32 [4096], P(('tm', 'pair')), may hold values from 0 to 262143, as said below
- pair_channels: int32 [2, 16384], P(None, 'pair'), may hold values from 0 to 255
Outputs:
- surface: float32 [64, 16384], P(None, 'pair')
Inputs may be any that keep to these rules, and one draw needn't show every extreme that they name: `hop_offsets`: hop p starts at a sample in p * 64 to p * 64 + 63.
All inputs are finite; a program needn't handle non-finite values.
Results may differ from a plain program's by a relative error of at most 0.000071.
Values sent between devices are 32-bit elements; how exact they have to be, the bound alone decides.
A program may use at most 64 MiB of HBM per device.

v0:
```python
import math

import jax
import jax.numpy as jnp
from jax import lax
from jax.sharding import PartitionSpec as P

NP = 256
Q = 64
STRIDE = 64


def shifted(array, axis, by):
    devices = lax.axis_size(axis)
    pairs = [(i, i + by) for i in range(devices) if 0 <= i + by < devices]
    return lax.ppermute(array, axis, pairs)


def joined_along(parts, dim):
    parts = jnp.moveaxis(parts, 0, dim)
    shape = parts.shape
    return parts.reshape(*shape[:dim], shape[dim] * shape[dim + 1], *shape[dim + 2 :])


def sent_to_all(array, axis):
    devices = lax.axis_size(axis)
    return lax.all_to_all(
        jnp.broadcast_to(array[None], (devices, *array.shape)), axis, 0, 0, tiled=True
    )


def gather_directly(array, axis, dim):
    return joined_along(sent_to_all(array, axis), dim)


def first_table():
    sample = jnp.arange(NP, dtype=jnp.int32)
    turns = sample[:, None] * sample[None, :] % NP
    angle = 2.0 * jnp.pi * turns.astype(jnp.float32) / NP
    window = 0.54 - 0.46 * jnp.cos(2.0 * jnp.pi * sample.astype(jnp.float32) / NP)
    gainval = 1.0 / jnp.sqrt(jnp.sum(window * window))
    weight = (window * gainval)[:, None]
    cosine = jnp.cos(angle) * weight
    sine = jnp.sin(angle) * weight
    upper = jnp.concatenate([cosine, -sine], axis=1)
    lower = jnp.concatenate([sine, cosine], axis=1)
    return jnp.concatenate([upper, lower], axis=0)


def second_table():
    sample = jnp.arange(Q, dtype=jnp.int32)
    turns = sample[:, None] * sample[None, :] % Q
    angle = 2.0 * jnp.pi * turns.astype(jnp.float32) / Q
    cosine = jnp.cos(angle) / math.sqrt(Q)
    sine = jnp.sin(angle) / math.sqrt(Q)
    upper = jnp.concatenate([cosine, sine], axis=1)
    lower = jnp.concatenate([-sine, cosine], axis=1)
    return jnp.concatenate([upper, lower], axis=0)


def cut_frames(extended, offsets, base):
    rows = offsets.shape[0]
    pieces = []
    for index in range(NP // STRIDE + 1):
        part_rows = extended[:, index * STRIDE : index * STRIDE + rows * STRIDE]
        pieces.append(part_rows.reshape(2, rows, STRIDE))
    segment = jnp.concatenate(pieces, axis=2)
    nominal = jnp.arange(rows, dtype=jnp.int32) * STRIDE
    jitter = offsets - base - nominal
    bit = 0
    while 1 << bit < STRIDE:
        step = 1 << bit
        moved = jnp.concatenate(
            [segment[:, :, step:], jnp.zeros((2, rows, step), segment.dtype)], axis=2
        )
        flagged = jitter >> bit & 1 == 1
        segment = jnp.where(flagged[None, :, None], moved, segment)
        bit = bit + 1
    return jnp.concatenate([segment[0, :, :NP], segment[1, :, :NP]], axis=1)


def channelize(extended, offsets, base):
    sample = jnp.arange(NP, dtype=jnp.int32)
    frames = cut_frames(extended, offsets, base)
    raw = jnp.dot(
        frames, first_table(), precision=lax.Precision.HIGHEST, preferred_element_type=jnp.float32
    )
    turns = sample[None, :] * (offsets[:, None] % NP) % NP
    theta = 2.0 * jnp.pi * turns.astype(jnp.float32) / NP
    cosine = jnp.cos(theta)
    sine = jnp.sin(theta)
    real_part = raw[:, :NP]
    imag_part = raw[:, NP:]
    return jnp.concatenate(
        [real_part * cosine + imag_part * sine, imag_part * cosine - real_part * sine], axis=1
    )


def two_sum(left, right):
    total = left[0] + right[0]
    back = total - left[0]
    error = left[0] - (total - back) + (right[0] - back)
    return (total, left[1] + error)


def shards(signal, hop_offsets, pair_channels):
    span = signal.shape[1]
    edge_part = shifted(signal[:, :NP], "tm", -1)
    extended = jnp.concatenate([signal, edge_part], axis=1)
    base = lax.axis_index("tm") * span
    all_offsets = gather_directly(hop_offsets, "pair", 0)
    spectra = channelize(extended, all_offsets, base)
    hop_count = spectra.shape[0]
    blocks = hop_count // Q
    local_pairs = pair_channels.shape[1]
    width = math.gcd(local_pairs, 512)
    grouped = pair_channels.reshape(2, local_pairs // width, width).transpose(1, 0, 2)
    table = second_table()
    channel_major = spectra.T

    def block_power(index):
        columns = jnp.concatenate([index[0], index[0] + NP, index[1], index[1] + NP])
        picked = jnp.take(channel_major, columns, axis=0)
        first_re = picked[:width]
        first_im = picked[width : 2 * width]
        second_re = picked[2 * width : 3 * width]
        second_im = picked[3 * width :]
        prod_re = first_re * second_re + first_im * second_im
        prod_im = first_im * second_re - first_re * second_im
        stacked = jnp.concatenate(
            [prod_re.reshape(width, blocks, Q), prod_im.reshape(width, blocks, Q)], axis=2
        )
        cyclic = jnp.einsum(
            "qh,pbh->pbq",
            table,
            stacked,
            precision=lax.Precision.HIGHEST,
            preferred_element_type=jnp.float32,
        )
        power = jnp.sum(cyclic * cyclic, axis=1)
        return power[:, :Q] + power[:, Q:]

    powers = lax.map(block_power, grouped)
    partial_power = powers.transpose(2, 0, 1).reshape(Q, local_pairs)
    devices = lax.axis_size("tm")
    total_blocks = blocks * devices
    received = lax.all_to_all(partial_power, "tm", split_axis=0, concat_axis=0, tiled=True)
    pieces = received.reshape(devices, Q // devices, local_pairs)
    zeros = jnp.zeros((Q // devices, local_pairs), jnp.float32)

    def absorb(carry, piece):
        return (two_sum(carry, (piece, zeros)), None)

    summed, unused = lax.scan(absorb, (zeros, zeros), pieces)
    finished = (summed[0] + summed[1]) / total_blocks
    return gather_directly(finished, "tm", 0)


def solution(mesh):
    return jax.shard_map(
        shards,
        mesh=mesh,
        in_specs=(P(None, "tm"), P(("tm", "pair")), P(None, "pair")),
        out_specs=P(None, "pair"),
        check_vma=False,
    )
```

profile of v0, /device:TPU:1, one launch (start us, length us, event | category | flops | bytes accessed | tf_op | source)
XLA Modules:
  0.0 103.8 jit_solution(2327456935706975326)
XLA Ops:
  0.7 1.3 %collective-permute-start = (f32[2,256]{1,0:T(2,128)S(1)}, f32[2,256]{1,0:T(2,128)S(1)}, u32[]{:S(2)}, u32[]{:S(2)}) collective-permute-start(f32[2,256]{1,0:T(2,128)S(1)} %slice.73), channel_id=1, source_target_pairs={{8,0},{16,8},{24,16},{32,24},{40,32},{48,40},{56,48},{64,56},{72,6... | collective-permute-start | bytes 6152 | tf_op jit(solution)/shard_map/ppermute | solution.py:16
  2.0 1.3 %broadcast_in_dim.85 = s32[8,1,32]{2,1,0:T(1,128)} broadcast(s32[32]{0:T(128)} %param.8), dimensions={2} | broadcast | bytes 1152 | tf_op jit(solution)/shard_map/broadcast_in_dim | solution.py:28
  3.2 6.0 %all-to-all-start = ((s32[8,1,32]{2,1,0:T(1,128)}), s32[8,1,32]{2,1,0:T(1,128)S(1)}, u32[]{:S(2)}, u32[]{:S(2)}) async-start(s32[8,1,32]{2,1,0:T(1,128)} %broadcast_in_dim.85), calls=%async_computation | async-start | bytes 8192 | tf_op jit(solution)/shard_map/all_to_all | solution.py:27
  9.2 0.9 constant_dynamic-update-slice_fusion.1
  11.8 1.1 %fusion.35 = (f32[256,256]{1,0:T(8,128)S(1)}, f32[256,256]{1,0:T(8,128)S(1)}, f32[256,256]{1,0:T(8,128)S(1)}) fusion(f32[256]{0:T(256)S(1)} %fusion.44), kind=kLoop, calls=%fused_computation.70 | loop fusion | flops 1114112 | bytes 787456 | tf_op jit(solution)/shard_map/neg | solution.py:45
  13.0 1.1 %reshape.311 = f32[2,256,64]{2,1,0:T(8,128)S(1)} reshape(f32[2,16384]{1,0:T(2,128)} %param.7) | data formatting | bytes 262144 | tf_op jit(solution)/shard_map/reshape | solution.py:66
  19.4 1.1 %fusion.10 = f32[256,512]{1,0:T(8,128)S(1)} fusion(f32[256,256]{1,0:T(8,128)S(1)} %get-tuple-element.126, f32[256,256]{1,0:T(8,128)S(1)} %get-tuple-element.125, f32[256,256]{1,0:T(8,128)S(1)} %get-tuple-element.124, f32[256,256]{1,0:T(8,128)S(1)} %get-tuple-element.112, f32[256,256]{1,0:T(8,128)S(1)} %get-tuple-element.111), kind=kOutput, calls=%fused_computation.26 | convolution fusion | flops 806223872 | bytes 1835008 | tf_op jit(solution)/shard_map/dot_general | solution.py:85
  20.5 1.3 %multiply_add_fusion.1 = (f32[256,256]{1,0:T(8,128)S(1)}, f32[256,256]{1,0:T(8,128)S(1)}) fusion(f32[256,512]{1,0:T(8,128)S(1)} %fusion.10, s32[256]{0:T(256)S(1)} %and_select_fusion), kind=kLoop, calls=%fused_computation.59 | loop fusion | flops 1310720 | bytes 1049600 | tf_op jit(solution)/shard_map/add | solution.py:95
  22.1 43.8 %while.23 = (s32[]{:T(128)}, f32[4,512,64]{2,1,0:T(8,128)}, s32[4,2,512]{2,1,0:T(2,128)}, f32[512,256]{1,0:T(8,128)S(1)}, f32[128,128]{1,0:T(8,128)S(1)}, /*index=5*/s32[]{:T(128)}, s32[]{:T(128)}, s32[]{}) while((s32[]{:T(128)}, f32[4,512,64]{2,1,0:T(8,128)}, s32[4,2,512]{2,1,0:T(2,128)}, f32[512,256]{1,0:T(8,128)S(1)}, ...), condition=%wide.region_3.4_spmd, body=%wide.region_1.3_spmd.sunk | while | flops 404751360 | bytes 17699432 | solution.py:143
  22.9 6.6 %gather_fusion = f32[2048,256]{1,0:T(8,128)S(1)} fusion(f32[512,256]{1,0:T(8,128)S(1)} %get-tuple-element.220, s32[2048]{0:T(1024)S(1)} %broadcast_clamp_fusion.2), kind=kCustom, calls=%fused_computation.clone.1 | custom fusion | bytes 4202496 | tf_op jit(solution)/shard_map/while/body/eval_jaxpr/jit(_take)/gather | solution.py:123
  31.1 1.0 %fusion.54 = f32[512,128]{1,0:T(8,128)S(1)} fusion(f32[512,4,64]{2,0,1:T(8,128)S(1)} %copy.17, f32[512,4,64]{2,0,1:T(8,128)S(1)} %copy.19, f32[128,128]{1,0:T(8,128)S(1)} %get-tuple-element.221), kind=kOutput, calls=%fused_computation.2.clone.1 | convolution fusion | flops 403374080 | bytes 1376256 | tf_op jit(solution)/shard_map/while/body/eval_jaxpr/qh,pbh->pbq/dot_general | solution.py:133
  33.9 6.6 %gather_fusion = f32[2048,256]{1,0:T(8,128)S(1)} fusion(f32[512,256]{1,0:T(8,128)S(1)} %get-tuple-element.220, s32[2048]{0:T(1024)S(1)} %broadcast_clamp_fusion.2), kind=kCustom, calls=%fused_computation.clone.1 | custom fusion | bytes 4202496 | tf_op jit(solution)/shard_map/while/body/eval_jaxpr/jit(_take)/gather | solution.py:123
  42.1 1.0 %fusion.54 = f32[512,128]{1,0:T(8,128)S(1)} fusion(f32[512,4,64]{2,0,1:T(8,128)S(1)} %copy.17, f32[512,4,64]{2,0,1:T(8,128)S(1)} %copy.19, f32[128,128]{1,0:T(8,128)S(1)} %get-tuple-element.221), kind=kOutput, calls=%fused_computation.2.clone.1 | convolution fusion | flops 403374080 | bytes 1376256 | tf_op jit(solution)/shard_map/while/body/eval_jaxpr/qh,pbh->pbq/dot_general | solution.py:133
  44.8 6.6 %gather_fusion = f32[2048,256]{1,0:T(8,128)S(1)} fusion(f32[512,256]{1,0:T(8,128)S(1)} %get-tuple-element.220, s32[2048]{0:T(1024)S(1)} %broadcast_clamp_fusion.2), kind=kCustom, calls=%fused_computation.clone.1 | custom fusion | bytes 4202496 | tf_op jit(solution)/shard_map/while/body/eval_jaxpr/jit(_take)/gather | solution.py:123
  53.0 1.1 %fusion.54 = f32[512,128]{1,0:T(8,128)S(1)} fusion(f32[512,4,64]{2,0,1:T(8,128)S(1)} %copy.17, f32[512,4,64]{2,0,1:T(8,128)S(1)} %copy.19, f32[128,128]{1,0:T(8,128)S(1)} %get-tuple-element.221), kind=kOutput, calls=%fused_computation.2.clone.1 | convolution fusion | flops 403374080 | bytes 1376256 | tf_op jit(solution)/shard_map/while/body/eval_jaxpr/qh,pbh->pbq/dot_general | solution.py:133
  55.8 6.6 %gather_fusion = f32[2048,256]{1,0:T(8,128)S(1)} fusion(f32[512,256]{1,0:T(8,128)S(1)} %get-tuple-element.220, s32[2048]{0:T(1024)S(1)} %broadcast_clamp_fusion.2), kind=kCustom, calls=%fused_computation.clone.1 | custom fusion | bytes 4202496 | tf_op jit(solution)/shard_map/while/body/eval_jaxpr/jit(_take)/gather | solution.py:123
  64.0 1.0 %fusion.54 = f32[512,128]{1,0:T(8,128)S(1)} fusion(f32[512,4,64]{2,0,1:T(8,128)S(1)} %copy.17, f32[512,4,64]{2,0,1:T(8,128)S(1)} %copy.19, f32[128,128]{1,0:T(8,128)S(1)} %get-tuple-element.221), kind=kOutput, calls=%fused_computation.2.clone.1 | convolution fusion | flops 403374080 | bytes 1376256 | tf_op jit(solution)/shard_map/while/body/eval_jaxpr/qh,pbh->pbq/dot_general | solution.py:133
  65.9 1.6 %copy.11 = f32[64,4,512]{2,1,0:T(4,128)S(1)} copy(f32[64,4,512]{0,2,1:T(8,128)} %bitcast.16) | data formatting | bytes 1048576 | tf_op jit(solution)/shard_map/transpose | solution.py:144
  67.5 1.2 %all_to_all.14 = f32[16,4,2048]{2,1,0:T(4,128)} reshape(f32[64,4,512]{2,1,0:T(4,128)S(1)} %copy.11) | data formatting | bytes 1048576 | tf_op jit(solution)/shard_map/all_to_all | solution.py:147
  68.7 8.8 %all-to-all-start.1 = ((f32[16,4,2048]{2,1,0:T(4,128)}), f32[16,4,2048]{2,1,0:T(4,128)S(1)}, u32[]{:S(2)}, u32[]{:S(2)}) async-start(f32[16,4,2048]{2,1,0:T(4,128)} %all_to_all.14), calls=%async_computation.1 | async-start | bytes 1048576 | tf_op jit(solution)/shard_map/all_to_all | solution.py:147
  77.5 10.8 %all-to-all-done.1 = f32[16,4,2048]{2,1,0:T(4,128)S(1)} async-done(((f32[16,4,2048]{2,1,0:T(4,128)}), f32[16,4,2048]{2,1,0:T(4,128)S(1)}, u32[]{:S(2)}, u32[]{:S(2)}) %all-to-all-start.1) | async-done | bytes 524320 | tf_op jit(solution)/shard_map/all_to_all | solution.py:147
  88.3 1.0 while.24
  89.4 13.4 %all_to_all.20 = f32[16,4,2048]{2,1,0:T(4,128)S(1)} all-to-all(f32[16,4,2048]{2,1,0:T(4,128)S(1)} %broadcast_in_dim.92), channel_id=1, replica_groups=mesh['tm'=16,'pair'=8] {'tm'}, dimensions={0} | all-to-all | bytes 1048576 | tf_op jit(solution)/shard_map/all_to_all | solution.py:27
  102.8 1.0 reshape.316
  (105 shorter events, 20.9 us)
Async XLA Ops:
  0.7 14.7 %collective-permute-start = (f32[2,256]{1,0:T(2,128)S(1)}, f32[2,256]{1,0:T(2,128)S(1)}, u32[]{:S(2)}, u32[]{:S(2)}) collective-permute-start(f32[2,256]{1,0:T(2,128)S(1)} %slice.73), channel_id=1, source_target_pairs={{8,0},{16,8},{24,16},{32,24},{40,32},{48,40},{56,48},{64,56},{72,6... | collective-permute-start | bytes 6152 | tf_op jit(solution)/shard_map/ppermute | solution.py:16
  3.2 10.9 %all-to-all-start = ((s32[8,1,32]{2,1,0:T(1,128)}), s32[8,1,32]{2,1,0:T(1,128)S(1)}, u32[]{:S(2)}, u32[]{:S(2)}) async-start(s32[8,1,32]{2,1,0:T(1,128)} %broadcast_in_dim.85), calls=%async_computation | async-start | bytes 8192 | tf_op jit(solution)/shard_map/all_to_all | solution.py:27
  68.7 19.6 %all-to-all-start.1 = ((f32[16,4,2048]{2,1,0:T(4,128)}), f32[16,4,2048]{2,1,0:T(4,128)S(1)}, u32[]{:S(2)}, u32[]{:S(2)}) async-start(f32[16,4,2048]{2,1,0:T(4,128)} %all_to_all.14), calls=%async_computation.1 | async-start | bytes 1048576 | tf_op jit(solution)/shard_map/all_to_all | solution.py:147
where the time goes:
time: 105 us; the launch traced here: 104 us
  local copies, waits for them, and re-layouts  45.6 us (43%)
  starting transfers between devices  16 us (15%)
  blocking collectives  13.4 us (13%)
  other arithmetic  11.3 us (11%)
  waiting for transfers between devices  10.8 us (10%)
  matrix products  5.24 us (5%)
    gather x4, local copies, waits for them, and re-layouts, block_power(): picked = jnp.take(channel_major, columns, axis=0)  26.6 us
    all_to_all x1, blocking collectives, sent_to_all(): lax.all_to_all(jnp.broadcast_to(array[None], (devices, *array.shape)), ax...  13.4 us
    all_to_all x1, waiting for transfers between devices, shards(): lax.all_to_all(partial_power, 'tm', split_axis=0, concat_axis=0, tiled=True)  10.8 us
    all_to_all x1, starting transfers between devices, shards(): lax.all_to_all(partial_power, 'tm', split_axis=0, concat_axis=0, tiled=True)  8.78 us
    all_to_all x1, starting transfers between devices, sent_to_all(): lax.all_to_all(jnp.broadcast_to(array[None], (devices, *array.shape)), ax...  5.96 us
    dot_general x4, matrix products, block_power(): jnp.einsum('qh,pbh->pbq', table, stacked, precision=lax.Precision.HIGHEST...  4.19 us
    dynamic_update_slice x4, other arithmetic, shards(): powers = lax.map(block_power, grouped)  3.37 us
    slice x4, local copies, waits for them, and re-layouts, block_power(): index[0]  3.08 us
  transfers between devices with their start and end apart: 3, of which 1 were waited for; matrix products, arithmetic and copies ran while one was open for 7% of the time, Pallas kernels for 0%

commit v1 on v0

v1 whole, which is shorter than its diff:
```python
import numpy as np

import jax
import jax.numpy as jnp
from jax import lax
from jax.experimental import pallas as pl
from jax.experimental.pallas import tpu as pltpu
from jax.sharding import PartitionSpec as P

NP = 256
Q = 64
TM = 16
PAIR = 8
HOPS = 256
PAIRS = 2048
WIDTH = 256
CHUNKS = PAIRS // WIDTH
SLICE = PAIRS // TM
BLOCKS = HOPS // Q
MESH = pl.DeviceIdType.MESH
F32 = jnp.float32
BF16 = jnp.bfloat16


def split(table):
    high = table.astype(np.float32).astype(BF16)
    low = (table - high.astype(np.float64)).astype(np.float32).astype(BF16)
    return high, low


def tables():
    sample = np.arange(NP // 2)
    out = []
    for odd in (0, 1):
        turns = np.outer(sample, 2 * sample + odd) % NP
        angle = 2.0 * np.pi * turns / NP
        cosine, sine = np.cos(angle), np.sin(angle)
        table = np.block([[cosine, -sine], [sine, cosine]])
        out.extend(split(table))
    hop = (4 * np.arange(Q // 4)[None, :] + np.arange(4)[:, None]).reshape(Q)
    turns = np.outer(np.arange(Q), hop) % Q
    angle = 2.0 * np.pi * turns / Q
    cosine, sine = np.cos(angle) / 8.0, np.sin(angle) / 8.0
    high, low = split(np.block([[cosine, sine], [-sine, cosine]]))
    upper = np.concatenate([high, high], axis=1)
    lower = np.concatenate([low, np.zeros_like(low)], axis=1)
    out.append(np.concatenate([upper, lower], axis=0))
    return np.stack(out)


def window_rows():
    sample = np.arange(NP)
    angle = 2.0 * np.pi * sample / NP
    window = 0.54 - 0.46 * np.cos(angle)
    gain = 1.0 / np.sqrt(np.sum(window * window))
    rows = np.zeros((8, NP))
    rows[0] = 0.54 * gain
    rows[1] = -0.46 * gain * np.cos(angle)
    rows[2] = -0.46 * gain * np.sin(angle)
    return rows.astype(np.float32)


def high_low(value):
    high = value.astype(BF16)
    return high, (value - high.astype(F32)).astype(BF16)


def dot(left, right):
    return jnp.dot(left, right, preferred_element_type=F32)


def kernel(
    sig_ref, off_ref, pc_ref, win_ref, tab_hbm, out_ref,
    rows_ref, edge_ref, msg_ref, tab_ref, grid_ref, spec_ref, hot_ref,
    part_ref, recv_ref, done_ref,
    tab_sem, edge_send, edge_recv, msg_send, msg_recv, part_send, part_recv, done_send, done_recv,
):
    tm = lax.axis_index("tm")
    pr = lax.axis_index("pair")

    barrier = pltpu.get_barrier_semaphore()

    def greet_tm(step, carry):
        peer = lax.rem(tm + step, TM)
        pl.semaphore_signal(barrier, inc=1, device_id=(peer, pr), device_id_type=MESH)
        return carry

    def greet_pair(step, carry):
        peer = lax.rem(pr + step, PAIR)
        pl.semaphore_signal(barrier, inc=1, device_id=(tm, peer), device_id_type=MESH)
        return carry

    lax.fori_loop(1, TM, greet_tm, 0)
    lax.fori_loop(1, PAIR, greet_pair, 0)

    tab_copy = pltpu.make_async_copy(tab_hbm, tab_ref, tab_sem)
    tab_copy.start()

    lane = lax.broadcasted_iota(jnp.int32, (8, 128), 1)
    row32 = lax.broadcasted_iota(jnp.int32, (8, 32), 0)
    lane32 = lax.broadcasted_iota(jnp.int32, (8, 32), 1)
    shift = (off_ref[...] & (NP - 1)).astype(F32)
    shift = jnp.broadcast_to(shift, (8, 32))
    value = jnp.zeros((8, 128), F32)
    for u in range(4):
        column = jnp.sum(jnp.where(lane32 == 4 * row32 + u, shift, 0.0), axis=1, keepdims=True)
        value = jnp.where((lane & 3) == u, column, value)
    theta = value * (2.0 * np.pi / NP)
    value = jnp.where(lane < 4, value, jnp.where(lane < 8, jnp.cos(theta), jnp.sin(theta)))
    msg_ref[pr] = value

    for group in range(HOPS // 2):
        rows_ref[2 * group : 2 * group + 2, :] = sig_ref[:, 128 * group : 128 * (group + 1)]

    pl.semaphore_wait(barrier, TM + PAIR - 2)

    def edge_copy():
        return pltpu.make_async_remote_copy(
            src_ref=sig_ref.at[:, pl.ds(0, NP)],
            dst_ref=edge_ref,
            send_sem=edge_send,
            recv_sem=edge_recv,
            device_id=(lax.rem(tm + TM - 1, TM), pr),
            device_id_type=MESH,
        )

    def msg_copy(slot, peer):
        return pltpu.make_async_remote_copy(
            src_ref=msg_ref.at[slot],
            dst_ref=msg_ref.at[slot],
            send_sem=msg_send.at[peer],
            recv_sem=msg_recv.at[slot],
            device_id=(tm, peer),
            device_id_type=MESH,
        )

    edge_copy().start()

    def send_msg(step, carry):
        msg_copy(pr, lax.rem(pr + step, PAIR)).start()
        return carry

    lax.fori_loop(1, PAIR, send_msg, 0)

    channel = lax.broadcasted_iota(jnp.int32, (NP, WIDTH), 0)

    def build_hot(chunk, carry):
        start = pl.multiple_of(chunk * WIDTH, WIDTH)
        for side in range(2):
            index = pc_ref[side : side + 1, pl.ds(start, WIDTH)]
            index = (index >> 1) + (index & 1) * (NP // 2)
            hot_ref[chunk, side] = jnp.where(channel == index, 1.0, 0.0).astype(BF16)
        return carry

    lax.fori_loop(0, CHUNKS, build_hot, 0)
    tab_copy.wait()

    edge_copy().wait_recv()

    def wait_msg(step, carry):
        slot = lax.rem(pr + step, PAIR)
        msg_copy(slot, slot).wait_recv()
        return carry

    lax.fori_loop(1, PAIR, wait_msg, 0)

    last = tm == TM - 1
    edge = jnp.where(last, 0.0, edge_ref[...])
    rows_ref[HOPS : HOPS + 2, :] = edge[:, :128]
    rows_ref[HOPS + 2 : HOPS + 4, :] = edge[:, 128:]

    messages = msg_ref[...].reshape(Q, 128)
    column = lax.broadcasted_iota(jnp.int32, (Q, 128), 1).astype(F32)

    def samples(part, half, ahead):
        return rows_ref[pl.ds(2 * half + part + 4 * ahead, Q, stride=4), :]

    for u in range(4):
        start = messages[:, u : u + 1]
        cosine = messages[:, 4 + u : 5 + u]
        sine = messages[:, 8 + u : 9 + u]
        halves = []
        for half in range(2):
            lanes = slice(128 * half, 128 * half + 128)
            weight = win_ref[0:1, lanes] + cosine * win_ref[1:2, lanes] + sine * win_ref[2:3, lanes]
            here = column + 128.0 * half >= start
            halves.append(
                [jnp.where(here, samples(part, half, 0), samples(part, half, 1)) * weight for part in range(2)]
            )
        for sign in range(2):
            for part in range(2):
                left, right = halves[0][part], halves[1][part]
                high, low = high_low(left - right if sign else left + right)
                grid_ref[sign, 0, u * Q : (u + 1) * Q, 128 * part : 128 * (part + 1)] = high
                grid_ref[sign, 1, u * Q : (u + 1) * Q, 128 * part : 128 * (part + 1)] = low

    for odd in range(2):
        high, low = grid_ref[odd, 0], grid_ref[odd, 1]
        result = dot(high, tab_ref[2 * odd]) + dot(low, tab_ref[2 * odd]) + dot(high, tab_ref[2 * odd + 1])
        high, low = high_low(result)
        for u in range(4):
            for block in range(BLOCKS):
                source = slice(u * Q + 16 * block, u * Q + 16 * block + 16)
                for part in range(2):
                    target = slice(block * 128 + part * 64 + 16 * u, block * 128 + part * 64 + 16 * u + 16)
                    lanes = slice(128 * part, 128 * part + 128)
                    spec_ref[target, 128 * odd : 128 * odd + 128] = high[source, lanes]
                    spec_ref[target, 256 + 128 * odd : 384 + 128 * odd] = low[source, lanes]

    def part_copy(slot, owner):
        return pltpu.make_async_remote_copy(
            src_ref=part_ref.at[owner],
            dst_ref=recv_ref.at[slot],
            send_sem=part_send.at[owner],
            recv_sem=part_recv.at[slot],
            device_id=(owner, pr),
            device_id_type=MESH,
        )

    def compute(step, carry):
        chunk = lax.rem(tm // 2 + 1 + step, CHUNKS)
        pick_a = hot_ref[chunk, 0]
        pick_b = hot_ref[chunk, 1]
        first = dot(spec_ref[:, :NP], pick_a) + dot(spec_ref[:, NP:], pick_a)
        second = dot(spec_ref[:, :NP], pick_b) + dot(spec_ref[:, NP:], pick_b)
        power = jnp.zeros((Q, WIDTH), F32)
        for block in range(BLOCKS):
            base = block * 2 * Q
            first_re, first_im = first[base : base + Q], first[base + Q : base + 2 * Q]
            second_re, second_im = second[base : base + Q], second[base + Q : base + 2 * Q]
            re_high, re_low = high_low(first_re * second_re + first_im * second_im)
            im_high, im_low = high_low(first_im * second_re - first_re * second_im)
            stacked = jnp.concatenate([re_high, im_high, re_low, im_low], axis=0)
            both = dot(tab_ref[4], stacked)
            cyclic = both[: 2 * Q] + both[2 * Q :]
            square = cyclic * cyclic
            power = power + square[:Q] + square[Q:]
        for half in range(2):
            owner = 2 * chunk + half
            part_ref[owner] = power[:, half * SLICE : (half + 1) * SLICE]

            @pl.when(owner != tm)
            def send():
                part_copy(tm, owner).start()

        return carry

    lax.fori_loop(0, CHUNKS, compute, 0)

    def absorb(step, total):
        slot = lax.rem(tm + step, TM)
        part_copy(slot, slot).wait_recv()
        return total + recv_ref[slot]

    total = lax.fori_loop(1, TM, absorb, part_ref[tm])
    done_ref[tm] = total * (1.0 / Q)

    def done_copy(slot, peer):
        return pltpu.make_async_remote_copy(
            src_ref=done_ref.at[slot],
            dst_ref=done_ref.at[slot],
            send_sem=done_send.at[peer],
            recv_sem=done_recv.at[slot],
            device_id=(peer, pr),
            device_id_type=MESH,
        )

    def send_done(step, carry):
        done_copy(tm, lax.rem(tm + step, TM)).start()
        return carry

    lax.fori_loop(1, TM, send_done, 0)

    def wait_done(step, carry):
        slot = lax.rem(tm + step, TM)
        done_copy(slot, slot).wait_recv()
        return carry

    lax.fori_loop(1, TM, wait_done, 0)
    for slot in range(TM):
        out_ref[:, SLICE * slot : SLICE * (slot + 1)] = done_ref[slot]

    edge_copy().wait_send()

    def drain_msg(step, carry):
        msg_copy(pr, lax.rem(pr + step, PAIR)).wait_send()
        return carry

    def drain_tm(step, carry):
        peer = lax.rem(tm + step, TM)
        part_copy(tm, peer).wait_send()
        done_copy(tm, peer).wait_send()
        return carry

    lax.fori_loop(1, PAIR, drain_msg, 0)
    lax.fori_loop(1, TM, drain_tm, 0)


def shards(signal, hop_offsets, pair_channels):
    vmem = pl.BlockSpec(memory_space=pltpu.VMEM)
    return pl.pallas_call(
        kernel,
        out_shape=jax.ShapeDtypeStruct((Q, PAIRS), F32),
        in_specs=[vmem, vmem, vmem, vmem, pl.BlockSpec(memory_space=pl.ANY)],
        out_specs=vmem,
        scratch_shapes=[
            pltpu.VMEM((HOPS + 8, 128), F32),
            pltpu.VMEM((2, NP), F32),
            pltpu.VMEM((PAIR, 8, 128), F32),
            pltpu.VMEM((5, NP, NP), BF16),
            pltpu.VMEM((2, 2, HOPS, NP), BF16),
            pltpu.VMEM((2 * HOPS, 2 * NP), BF16),
            pltpu.VMEM((CHUNKS, 2, NP, WIDTH), BF16),
            pltpu.VMEM((TM, Q, SLICE), F32),
            pltpu.VMEM((TM, Q, SLICE), F32),
            pltpu.VMEM((TM, Q, SLICE), F32),
            pltpu.SemaphoreType.DMA,
            pltpu.SemaphoreType.DMA,
            pltpu.SemaphoreType.DMA,
            pltpu.SemaphoreType.DMA((PAIR,)),
            pltpu.SemaphoreType.DMA((PAIR,)),
            pltpu.SemaphoreType.DMA((TM,)),
            pltpu.SemaphoreType.DMA((TM,)),
            pltpu.SemaphoreType.DMA((TM,)),
            pltpu.SemaphoreType.DMA((TM,)),
        ],
        compiler_params=pltpu.CompilerParams(
            collective_id=0, has_side_effects=True, vmem_limit_bytes=48 * 1024 * 1024
        ),
    )(
        signal,
        hop_offsets.reshape(1, HOPS // PAIR),
        pair_channels,
        jnp.asarray(window_rows()),
        jnp.asarray(tables()),
    )


def solution(mesh):
    return jax.shard_map(
        shards,
        mesh=mesh,
        in_specs=(P(None, "tm"), P(("tm", "pair")), P(None, "pair")),
        out_specs=P(None, "pair"),
        check_vma=False,
    )
```

time: 105 us -> 38.1 us (0.36)
  local copies, waits for them, and re-layouts: 45.6 us -> 4.85 us
  Pallas kernels: 0 us -> 33 us
  starting transfers between devices: 16 us -> 0 us
  blocking collectives: 13.4 us -> 0 us
  other arithmetic: 11.3 us -> 0 us
  waiting for transfers between devices: 10.8 us -> 0 us
  matrix products: 5.24 us -> 0 us
    pallas_call x0 -> x1, Pallas kernels: none -> 33 us  [shards(): pl.pallas_call(kernel, out_shape=jax.ShapeDtypeStruct((Q, PAIRS), F32), i...]
    gather x4 -> x0, local copies, waits for them, and re-layouts: 26.6 us -> none  [block_power(): picked = jnp.take(channel_major, columns, axis=0)]
    all_to_all x2 -> x0, starting transfers between devices: 14.7 us -> none  [the longest x1 8.78 us: shards(): lax.all_to_all(partial_power, 'tm', split_axis=0, concat_axis=0, tiled=True)]
    all_to_all x1 -> x0, blocking collectives: 13.4 us -> none  [sent_to_all(): lax.all_to_all(jnp.broadcast_to(array[None], (devices, *array.shape)), ax...]
    all_to_all x2 -> x0, waiting for transfers between devices: 10.8 us -> none  [the longest x1 10.8 us: shards(): lax.all_to_all(partial_power, 'tm', split_axis=0, concat_axis=0, tiled=True)]
    slice x12 -> x0, local copies, waits for them, and re-layouts: 5.71 us -> none  [the longest x4 3.08 us: block_power(): index[0]]
    reshape x15 -> x0, local copies, waits for them, and re-layouts: 5.61 us -> none  [the longest x5 1.94 us: cut_frames(): pieces.append(part_rows.reshape(2, rows, STRIDE))]
    dot_general x5 -> x0, matrix products: 5.24 us -> none  [the longest x4 4.19 us: block_power(): jnp.einsum('qh,pbh->pbq', table, stacked, precision=lax.Precision.HIGHEST...]
  transfers between devices with their start and end apart: 3 -> 0, of which waited for: 1 -> 0; matrix products, arithmetic and copies ran while one was open for 7% -> 0% of each run, Pallas kernels for 0% -> 0%
where the time goes in v1:
time: 38.1 us; the launch traced here: 37.9 us
  Pallas kernels  33 us (87%)
  local copies, waits for them, and re-layouts  4.85 us (13%)
    pallas_call x1, Pallas kernels, shards(): pl.pallas_call(kernel, out_shape=jax.ShapeDtypeStruct((Q, PAIRS), F32), i...  33 us
    unnamed x11, local copies, waits for them, and re-layouts  4.85 us

profile of v1, /device:TPU:1, one launch (start us, length us, event | category | flops | bytes accessed | tf_op | source)
XLA Modules:
  0.0 37.9 jit_solution(12831917086160373291)
XLA Ops:
  0.0 0.0 copy-start.4
  0.0 0.7 %copy-done.4 = s32[32]{0:T(128)S(1)} copy-done((s32[32]{0:T(128)S(1)}, s32[32]{0:T(128)}, u32[]{:S(2)}) %copy-start.4) | copy-done | bytes 152
  0.7 0.0 copy-start
  0.7 1.1 %copy-done = bf16[5,256,256]{2,1,0:T(8,128)(2,1)S(1)} copy-done((bf16[5,256,256]{2,1,0:T(8,128)(2,1)S(1)}, bf16[5,256,256]{2,1,0:T(8,128)(2,1)}, u32[]{:S(2)}) %copy-start) | copy-done | bytes 655384
  1.7 0.0 copy-start.1
  1.7 0.9 %copy-done.1 = f32[2,16384]{1,0:T(2,128)S(1)} copy-done((f32[2,16384]{1,0:T(2,128)S(1)}, f32[2,16384]{1,0:T(2,128)}, u32[]{:S(2)}) %copy-start.1) | copy-done | bytes 131096
  2.6 0.0 copy-start.2
  2.7 0.7 %copy-done.2 = s32[2,2048]{1,0:T(2,128)S(1)} copy-done((s32[2,2048]{1,0:T(2,128)S(1)}, s32[2,2048]{1,0:T(2,128)}, u32[]{:S(2)}) %copy-start.2) | copy-done | bytes 16408
  3.4 0.0 copy-start.3
  3.4 0.7 %copy-done.3 = f32[8,256]{1,0:T(8,128)S(1)} copy-done((f32[8,256]{1,0:T(8,128)S(1)}, f32[8,256]{1,0:T(8,128)}, u32[]{:S(2)}) %copy-start.3) | copy-done | bytes 8216
  4.1 33.0 %shard_map.55 = f32[64,2048]{1,0:T(8,128)S(1)} custom-call(f32[2,16384]{1,0:T(2,128)S(1)} %copy-done.1, s32[1,32]{1,0:T(1,128)S(1)} %bitcast.1, s32[2,2048]{1,0:T(2,128)S(1)} %copy-done.2, f32[8,256]{1,0:T(8,128)S(1)} %copy-done.3, bf16[5,256,256]{2,1,0:T(8,128)(2,1)S(1)} %copy-done), custom_call_target="tpu_custom_call" | custom-call | tf_op jit(solution)/shard_map/pallas_call | solution.py:301
  37.1 0.8 %copy.7 = f32[64,2048]{1,0:T(8,128)} copy(f32[64,2048]{1,0:T(8,128)S(1)} %shard_map.55) | data formatting | bytes 1048576
Async XLA Ops:
  0.0 0.7 %copy-start.4 = (s32[32]{0:T(128)S(1)}, s32[32]{0:T(128)}, u32[]{:S(2)}) copy-start(s32[32]{0:T(128)} %param.6) | copy-start | bytes 388
  0.7 1.1 %copy-start = (bf16[5,256,256]{2,1,0:T(8,128)(2,1)S(1)}, bf16[5,256,256]{2,1,0:T(8,128)(2,1)}, u32[]{:S(2)}) copy-start(bf16[5,256,256]{2,1,0:T(8,128)(2,1)} %constant.5.clone.tab_hbm) | copy-start | bytes 1966084
  1.7 0.9 %copy-start.1 = (f32[2,16384]{1,0:T(2,128)S(1)}, f32[2,16384]{1,0:T(2,128)}, u32[]{:S(2)}) copy-start(f32[2,16384]{1,0:T(2,128)} %sig_ref.1) | copy-start | bytes 393220
  2.6 0.7 %copy-start.2 = (s32[2,2048]{1,0:T(2,128)S(1)}, s32[2,2048]{1,0:T(2,128)}, u32[]{:S(2)}) copy-start(s32[2,2048]{1,0:T(2,128)} %pc_ref.1) | copy-start | bytes 49156
  3.4 0.7 %copy-start.3 = (f32[8,256]{1,0:T(8,128)S(1)}, f32[8,256]{1,0:T(8,128)}, u32[]{:S(2)}) copy-start(f32[8,256]{1,0:T(8,128)} %constant.4.clone.win_ref) | copy-start | bytes 24580

commit v2 on v1

v2 whole, which is shorter than its diff:
```python
import numpy as np

import jax
import jax.numpy as jnp
from jax import lax
from jax.experimental import pallas as pl
from jax.experimental.pallas import tpu as pltpu
from jax.sharding import PartitionSpec as P

NP = 256
Q = 64
TM = 16
PAIR = 8
HOPS = 256
PAIRS = 2048
WIDTH = 256
CHUNKS = PAIRS // WIDTH
SLICE = PAIRS // TM
BLOCKS = HOPS // Q
MESH = pl.DeviceIdType.MESH
F32 = jnp.float32
BF16 = jnp.bfloat16


def split(table):
    high = table.astype(np.float32).astype(BF16)
    low = (table - high.astype(np.float64)).astype(np.float32).astype(BF16)
    return high, low


def tables():
    sample = np.arange(NP // 2)
    out = []
    for odd in (0, 1):
        turns = np.outer(sample, 2 * sample + odd) % NP
        angle = 2.0 * np.pi * turns / NP
        cosine, sine = np.cos(angle), np.sin(angle)
        table = np.block([[cosine, -sine], [sine, cosine]])
        out.extend(split(table))
    hop = (4 * np.arange(Q // 4)[None, :] + np.arange(4)[:, None]).reshape(Q)
    turns = np.outer(np.arange(Q), hop) % Q
    angle = 2.0 * np.pi * turns / Q
    cosine, sine = np.cos(angle) / 8.0, np.sin(angle) / 8.0
    high, low = split(np.block([[cosine, sine], [-sine, cosine]]))
    upper = np.concatenate([high, high], axis=1)
    lower = np.concatenate([low, np.zeros_like(low)], axis=1)
    out.append(np.concatenate([upper, lower], axis=0))
    return np.stack(out)


def window_rows():
    sample = np.arange(NP)
    angle = 2.0 * np.pi * sample / NP
    window = 0.54 - 0.46 * np.cos(angle)
    gain = 1.0 / np.sqrt(np.sum(window * window))
    rows = np.zeros((8, NP))
    rows[0] = 0.54 * gain
    rows[1] = -0.46 * gain * np.cos(angle)
    rows[2] = -0.46 * gain * np.sin(angle)
    return rows.astype(np.float32)


def high_low(value):
    high = value.astype(BF16)
    return high, (value - high.astype(F32)).astype(BF16)


def dot(left, right):
    return jnp.dot(left, right, preferred_element_type=F32)


def kernel(
    sig_hbm, off_hbm, pc_hbm, win_hbm, tab_hbm, out_ref,
    sig_ref, off_ref, pc_ref, win_ref, rows_ref, edge_ref, msg_ref, tab_ref, grid_ref, spec_ref, hot_ref,
    part_ref, recv_ref, done_ref,
    load_sem, edge_send, edge_recv, msg_send, msg_recv, part_send, part_recv, done_send, done_recv,
):
    tm = lax.axis_index("tm")
    pr = lax.axis_index("pair")

    with jax.named_scope("load_greet"):
        loads = [
            pltpu.make_async_copy(source, target, load_sem.at[index])
            for index, (source, target) in enumerate(
                (
                    (off_hbm, off_ref),
                    (sig_hbm, sig_ref),
                    (pc_hbm, pc_ref),
                    (win_hbm, win_ref),
                    (tab_hbm, tab_ref),
                )
            )
        ]
        for load in loads:
            load.start()
        barrier = pltpu.get_barrier_semaphore()

        def greet_tm(step, carry):
            peer = lax.rem(tm + step, TM)
            pl.semaphore_signal(barrier, inc=1, device_id=(peer, pr), device_id_type=MESH)
            return carry

        def greet_pair(step, carry):
            peer = lax.rem(pr + step, PAIR)
            pl.semaphore_signal(barrier, inc=1, device_id=(tm, peer), device_id_type=MESH)
            return carry

        lax.fori_loop(1, TM, greet_tm, 0)
        lax.fori_loop(1, PAIR, greet_pair, 0)

    with jax.named_scope("prep"):
        loads[0].wait()
        lane = lax.broadcasted_iota(jnp.int32, (8, 128), 1)
        row32 = lax.broadcasted_iota(jnp.int32, (8, 32), 0)
        lane32 = lax.broadcasted_iota(jnp.int32, (8, 32), 1)
        shift = (off_ref[...] & (NP - 1)).astype(F32)
        shift = jnp.broadcast_to(shift, (8, 32))
        value = jnp.zeros((8, 128), F32)
        for u in range(4):
            column = jnp.sum(jnp.where(lane32 == 4 * row32 + u, shift, 0.0), axis=1, keepdims=True)
            value = jnp.where((lane & 3) == u, column, value)
        theta = value * (2.0 * np.pi / NP)
        value = jnp.where(lane < 4, value, jnp.where(lane < 8, jnp.cos(theta), jnp.sin(theta)))
        msg_ref[pr] = value

        loads[1].wait()
        for group in range(HOPS // 2):
            rows_ref[2 * group : 2 * group + 2, :] = sig_ref[:, 128 * group : 128 * (group + 1)]

    with jax.named_scope("barrier"):
        pl.semaphore_wait(barrier, TM + PAIR - 2)

    with jax.named_scope("exchange_start"):
        def edge_copy():
            return pltpu.make_async_remote_copy(
                src_ref=sig_ref.at[:, pl.ds(0, NP)],
                dst_ref=edge_ref,
                send_sem=edge_send,
                recv_sem=edge_recv,
                device_id=(lax.rem(tm + TM - 1, TM), pr),
                device_id_type=MESH,
            )

        def msg_copy(slot, peer):
            return pltpu.make_async_remote_copy(
                src_ref=msg_ref.at[slot],
                dst_ref=msg_ref.at[slot],
                send_sem=msg_send.at[peer],
                recv_sem=msg_recv.at[slot],
                device_id=(tm, peer),
                device_id_type=MESH,
            )

        edge_copy().start()

        def send_msg(step, carry):
            msg_copy(pr, lax.rem(pr + step, PAIR)).start()
            return carry

        lax.fori_loop(1, PAIR, send_msg, 0)

    with jax.named_scope("hot"):
        channel = lax.broadcasted_iota(jnp.int32, (NP, WIDTH), 0)

        def build_hot(chunk, carry):
            start = pl.multiple_of(chunk * WIDTH, WIDTH)
            for side in range(2):
                index = pc_ref[side : side + 1, pl.ds(start, WIDTH)]
                index = (index >> 1) + (index & 1) * (NP // 2)
                hot_ref[chunk, side] = jnp.where(channel == index, 1.0, 0.0).astype(BF16)
            return carry

        loads[2].wait()
        lax.fori_loop(0, CHUNKS, build_hot, 0)
        loads[3].wait()
        loads[4].wait()

    with jax.named_scope("exchange_wait"):
        edge_copy().wait_recv()

        def wait_msg(step, carry):
            slot = lax.rem(pr + step, PAIR)
            msg_copy(slot, slot).wait_recv()
            return carry

        lax.fori_loop(1, PAIR, wait_msg, 0)

    with jax.named_scope("frames"):
        last = tm == TM - 1
        edge = jnp.where(last, 0.0, edge_ref[...])
        rows_ref[HOPS : HOPS + 2, :] = edge[:, :128]
        rows_ref[HOPS + 2 : HOPS + 4, :] = edge[:, 128:]

        messages = msg_ref[...].reshape(Q, 128)
        column = lax.broadcasted_iota(jnp.int32, (Q, 128), 1).astype(F32)

        def samples(part, half, ahead):
            return rows_ref[pl.ds(2 * half + part + 4 * ahead, Q, stride=4), :]

        for u in range(4):
            start = messages[:, u : u + 1]
            cosine = messages[:, 4 + u : 5 + u]
            sine = messages[:, 8 + u : 9 + u]
            halves = []
            for half in range(2):
                lanes = slice(128 * half, 128 * half + 128)
                weight = win_ref[0:1, lanes] + cosine * win_ref[1:2, lanes] + sine * win_ref[2:3, lanes]
                here = column + 128.0 * half >= start
                halves.append(
                    [jnp.where(here, samples(part, half, 0), samples(part, half, 1)) * weight for part in range(2)]
                )
            for sign in range(2):
                for part in range(2):
                    left, right = halves[0][part], halves[1][part]
                    high, low = high_low(left - right if sign else left + right)
                    grid_ref[sign, 0, u * Q : (u + 1) * Q, 128 * part : 128 * (part + 1)] = high
                    grid_ref[sign, 1, u * Q : (u + 1) * Q, 128 * part : 128 * (part + 1)] = low

    with jax.named_scope("spectra"):
        for odd in range(2):
            high, low = grid_ref[odd, 0], grid_ref[odd, 1]
            result = dot(high, tab_ref[2 * odd]) + dot(low, tab_ref[2 * odd]) + dot(high, tab_ref[2 * odd + 1])
            high, low = high_low(result)
            for u in range(4):
                for block in range(BLOCKS):
                    source = slice(u * Q + 16 * block, u * Q + 16 * block + 16)
                    for part in range(2):
                        target = slice(block * 128 + part * 64 + 16 * u, block * 128 + part * 64 + 16 * u + 16)
                        lanes = slice(128 * part, 128 * part + 128)
                        spec_ref[target, 128 * odd : 128 * odd + 128] = high[source, lanes]
                        spec_ref[target, 256 + 128 * odd : 384 + 128 * odd] = low[source, lanes]

    with jax.named_scope("main"):
        def part_copy(slot, owner):
            return pltpu.make_async_remote_copy(
                src_ref=part_ref.at[owner],
                dst_ref=recv_ref.at[slot],
                send_sem=part_send.at[owner],
                recv_sem=part_recv.at[slot],
                device_id=(owner, pr),
                device_id_type=MESH,
            )

        def compute(step, carry):
            chunk = lax.rem(tm // 2 + 1 + step, CHUNKS)
            pick_a = hot_ref[chunk, 0]
            pick_b = hot_ref[chunk, 1]
            first = dot(spec_ref[:, :NP], pick_a) + dot(spec_ref[:, NP:], pick_a)
            second = dot(spec_ref[:, :NP], pick_b) + dot(spec_ref[:, NP:], pick_b)
            power = jnp.zeros((Q, WIDTH), F32)
            for block in range(BLOCKS):
                base = block * 2 * Q
                first_re, first_im = first[base : base + Q], first[base + Q : base + 2 * Q]
                second_re, second_im = second[base : base + Q], second[base + Q : base + 2 * Q]
                re_high, re_low = high_low(first_re * second_re + first_im * second_im)
                im_high, im_low = high_low(first_im * second_re - first_re * second_im)
                stacked = jnp.concatenate([re_high, im_high, re_low, im_low], axis=0)
                both = dot(tab_ref[4], stacked)
                cyclic = both[: 2 * Q] + both[2 * Q :]
                square = cyclic * cyclic
                power = power + square[:Q] + square[Q:]
            for half in range(2):
                owner = 2 * chunk + half
                part_ref[owner] = power[:, half * SLICE : (half + 1) * SLICE]

                @pl.when(owner != tm)
                def send():
                    part_copy(tm, owner).start()

            return carry

        lax.fori_loop(0, CHUNKS, compute, 0)

    with jax.named_scope("absorb"):
        def absorb(step, total):
            slot = lax.rem(tm + step, TM)
            part_copy(slot, slot).wait_recv()
            return total + recv_ref[slot]

        total = lax.fori_loop(1, TM, absorb, part_ref[tm])
        done_ref[tm] = total * (1.0 / Q)

    with jax.named_scope("gather_send"):
        def done_copy(slot, peer):
            return pltpu.make_async_remote_copy(
                src_ref=done_ref.at[slot],
                dst_ref=done_ref.at[slot],
                send_sem=done_send.at[peer],
                recv_sem=done_recv.at[slot],
                device_id=(peer, pr),
                device_id_type=MESH,
            )

        def send_done(step, carry):
            done_copy(tm, lax.rem(tm + step, TM)).start()
            return carry

        lax.fori_loop(1, TM, send_done, 0)

    with jax.named_scope("gather_wait"):
        def wait_done(step, carry):
            slot = lax.rem(tm + step, TM)
            done_copy(slot, slot).wait_recv()
            return carry

        lax.fori_loop(1, TM, wait_done, 0)

    with jax.named_scope("output"):
        for slot in range(TM):
            out_ref[:, SLICE * slot : SLICE * (slot + 1)] = done_ref[slot]

    with jax.named_scope("drain"):
        edge_copy().wait_send()

        def drain_msg(step, carry):
            msg_copy(pr, lax.rem(pr + step, PAIR)).wait_send()
            return carry

        def drain_tm(step, carry):
            peer = lax.rem(tm + step, TM)
            part_copy(tm, peer).wait_send()
            done_copy(tm, peer).wait_send()
            return carry

        lax.fori_loop(1, PAIR, drain_msg, 0)
        lax.fori_loop(1, TM, drain_tm, 0)


def shards(signal, hop_offsets, pair_channels):
    vmem = pl.BlockSpec(memory_space=pltpu.VMEM)
    return pl.pallas_call(
        kernel,
        out_shape=jax.ShapeDtypeStruct((Q, PAIRS), F32),
        in_specs=[pl.BlockSpec(memory_space=pltpu.HBM)] * 5,
        out_specs=vmem,
        scratch_shapes=[
            pltpu.VMEM((2, HOPS * Q), F32),
            pltpu.VMEM((1, HOPS // PAIR), jnp.int32),
            pltpu.VMEM((2, PAIRS), jnp.int32),
            pltpu.VMEM((8, NP), F32),
            pltpu.VMEM((HOPS + 8, 128), F32),
            pltpu.VMEM((2, NP), F32),
            pltpu.VMEM((PAIR, 8, 128), F32),
            pltpu.VMEM((5, NP, NP), BF16),
            pltpu.VMEM((2, 2, HOPS, NP), BF16),
            pltpu.VMEM((2 * HOPS, 2 * NP), BF16),
            pltpu.VMEM((CHUNKS, 2, NP, WIDTH), BF16),
            pltpu.VMEM((TM, Q, SLICE), F32),
            pltpu.VMEM((TM, Q, SLICE), F32),
            pltpu.VMEM((TM, Q, SLICE), F32),
            pltpu.SemaphoreType.DMA((5,)),
            pltpu.SemaphoreType.DMA,
            pltpu.SemaphoreType.DMA,
            pltpu.SemaphoreType.DMA((PAIR,)),
            pltpu.SemaphoreType.DMA((PAIR,)),
            pltpu.SemaphoreType.DMA((TM,)),
            pltpu.SemaphoreType.DMA((TM,)),
            pltpu.SemaphoreType.DMA((TM,)),
            pltpu.SemaphoreType.DMA((TM,)),
        ],
        compiler_params=pltpu.CompilerParams(
            collective_id=0, has_side_effects=True, vmem_limit_bytes=48 * 1024 * 1024
        ),
    )(
        *(
            pltpu.with_memory_space_constraint(operand, pltpu.HBM)
            for operand in (
                signal,
                hop_offsets.reshape(1, HOPS // PAIR),
                pair_channels,
                jnp.asarray(window_rows()),
                jnp.asarray(tables()),
            )
        )
    )


def solution(mesh):
    return jax.shard_map(
        shards,
        mesh=mesh,
        in_specs=(P(None, "tm"), P(("tm", "pair")), P(None, "pair")),
        out_specs=P(None, "pair"),
        check_vma=False,
    )
```

time: 38.1 us -> 34 us (0.89)
  local copies, waits for them, and re-layouts: 4.85 us -> 0.8 us
    unnamed x11 -> x1, local copies, waits for them, and re-layouts: 4.85 us -> 0.8 us
where the time goes in v2:
time: 34 us; the launch traced here: 33.9 us
  Pallas kernels  33.1 us (97%)
  local copies, waits for them, and re-layouts  0.8 us (2%)
    pallas_call x1, Pallas kernels, shards(): pl.pallas_call(kernel, out_shape=jax.ShapeDtypeStruct((Q, PAIRS), F32), i...  33.1 us
    unnamed x1, local copies, waits for them, and re-layouts  0.8 us

profile of v2, /device:TPU:1, one launch (start us, length us, event | category | flops | bytes accessed | tf_op | source)
XLA Modules:
  0.0 33.9 jit_solution(4350089290766616247)
XLA Ops:
  0.0 33.1 %shard_map.55 = f32[64,2048]{1,0:T(8,128)S(1)} custom-call(f32[2,16384]{1,0:T(2,128)} %sig_hbm.1, s32[1,32]{1,0:T(1,128)} %bitcast.1, s32[2,2048]{1,0:T(2,128)} %pc_hbm.1, f32[8,256]{1,0:T(8,128)} %constant.4.clone.win_hbm, bf16[5,256,256]{2,1,0:T(8,128)(2,1)} %constant.5.clone.tab_hbm), custom_call_target="tpu_custom_call" | custom-call | tf_op jit(solution)/shard_map/pallas_call | solution.py:331
  33.1 0.8 %copy.7 = f32[64,2048]{1,0:T(8,128)} copy(f32[64,2048]{1,0:T(8,128)S(1)} %shard_map.55) | data formatting | bytes 1048576

commit v3 on v2

v3 whole, which is shorter than its diff:
```python
import numpy as np

import jax
import jax.numpy as jnp
from jax import lax
from jax.experimental import pallas as pl
from jax.experimental.pallas import tpu as pltpu
from jax.sharding import PartitionSpec as P

NP = 256
Q = 64
TM = 16
PAIR = 8
HOPS = 256
PAIRS = 2048
WIDTH = 256
CHUNKS = PAIRS // WIDTH
GROUPS = CHUNKS // 2
BLOCKS = HOPS // Q
MESH = pl.DeviceIdType.MESH
F32 = jnp.float32
BF16 = jnp.bfloat16


def split(table):
    high = table.astype(np.float32).astype(BF16)
    low = (table - high.astype(np.float64)).astype(np.float32).astype(BF16)
    return high, low


def tables():
    sample = np.arange(NP // 2)
    out = []
    for odd in (0, 1):
        turns = np.outer(sample, 2 * sample + odd) % NP
        angle = 2.0 * np.pi * turns / NP
        cosine, sine = np.cos(angle), np.sin(angle)
        table = np.block([[cosine, -sine], [sine, cosine]])
        out.extend(split(table))
    hop = (4 * np.arange(Q // 4)[None, :] + np.arange(4)[:, None]).reshape(Q)
    turns = np.outer(np.arange(Q), hop) % Q
    angle = 2.0 * np.pi * turns / Q
    cosine, sine = np.cos(angle) / 8.0, np.sin(angle) / 8.0
    high, low = split(np.block([[cosine, sine], [-sine, cosine]]))
    upper = np.concatenate([high, high], axis=1)
    lower = np.concatenate([low, np.zeros_like(low)], axis=1)
    out.append(np.concatenate([upper, lower], axis=0))
    return np.stack(out)


def window_rows():
    sample = np.arange(NP)
    angle = 2.0 * np.pi * sample / NP
    window = 0.54 - 0.46 * np.cos(angle)
    gain = 1.0 / np.sqrt(np.sum(window * window))
    rows = np.zeros((8, NP))
    rows[0] = 0.54 * gain
    rows[1] = -0.46 * gain * np.cos(angle)
    rows[2] = -0.46 * gain * np.sin(angle)
    return rows.astype(np.float32)


def high_low(value):
    high = value.astype(BF16)
    return high, (value - high.astype(F32)).astype(BF16)


def dot(left, right):
    return jnp.dot(left, right, preferred_element_type=F32)


def ring(distance, size):
    return min(distance, size - distance)


TM_STEPS = sorted(
    ((dz, dx) for dz in range(4) for dx in range(4) if dz or dx),
    key=lambda step: -(ring(step[0], 4) + ring(step[1], 4)),
)
PAIR_STEPS = sorted(
    ((dy, dc) for dy in range(4) for dc in range(2) if dy or dc),
    key=lambda step: -(2 * ring(step[0], 4) + step[1]),
)


def tm_peer(tm, step, sign=1):
    dz, dx = step
    return ((tm // 4 + sign * dz) % 4) * 4 + (tm % 4 + sign * dx) % 4


def pair_peer(pr, step, sign=1):
    dy, dc = step
    return ((pr // 2 + sign * dy) % 4) * 2 + (pr % 2 + dc) % 2


def exchange_kernel(
    sig_hbm, off_hbm, pc_hbm, win_hbm, tab_hbm,
    rows_ref, msg_ref, hot_ref, tab_ref, win_ref,
    sig_ref, off_ref, pc_ref, edge_ref,
    load_sem, edge_send, edge_recv, msg_send, msg_recv,
):
    tm = lax.axis_index("tm")
    pr = lax.axis_index("pair")
    before = (tm + TM - 1) % TM
    after = (tm + 1) % TM

    with jax.named_scope("load_greet"):
        barrier = pltpu.get_barrier_semaphore()
        for near, peer in ((tm > 0, before), (tm < TM - 1, after)):

            @pl.when(near)
            def greet():
                pl.semaphore_signal(barrier, inc=1, device_id=(peer, pr), device_id_type=MESH)

        for step in PAIR_STEPS:
            pl.semaphore_signal(barrier, inc=1, device_id=(tm, pair_peer(pr, step)), device_id_type=MESH)
        loads = [
            pltpu.make_async_copy(source, target, load_sem.at[index])
            for index, (source, target) in enumerate(
                (
                    (off_hbm, off_ref),
                    (sig_hbm, sig_ref),
                    (pc_hbm, pc_ref),
                    (win_hbm, win_ref),
                    (tab_hbm, tab_ref),
                )
            )
        ]
        for load in loads:
            load.start()

    with jax.named_scope("prep"):
        loads[0].wait()
        lane = lax.broadcasted_iota(jnp.int32, (8, 128), 1)
        row32 = lax.broadcasted_iota(jnp.int32, (8, 32), 0)
        lane32 = lax.broadcasted_iota(jnp.int32, (8, 32), 1)
        shift = (off_ref[...] & (NP - 1)).astype(F32)
        shift = jnp.broadcast_to(shift, (8, 32))
        value = jnp.zeros((8, 128), F32)
        for u in range(4):
            column = jnp.sum(jnp.where(lane32 == 4 * row32 + u, shift, 0.0), axis=1, keepdims=True)
            value = jnp.where((lane & 3) == u, column, value)
        theta = value * (2.0 * np.pi / NP)
        value = jnp.where(lane < 4, value, jnp.where(lane < 8, jnp.cos(theta), jnp.sin(theta)))
        msg_ref[pr] = value
        loads[1].wait()

    with jax.named_scope("barrier"):
        ends = jnp.where((tm == 0) | (tm == TM - 1), 1, 2)
        pl.semaphore_wait(barrier, PAIR - 1 + ends)

    with jax.named_scope("exchange_start"):
        def msg_copy(index, slot):
            return pltpu.make_async_remote_copy(
                src_ref=msg_ref.at[slot],
                dst_ref=msg_ref.at[slot],
                send_sem=msg_send,
                recv_sem=msg_recv,
                device_id=(tm, pair_peer(pr, PAIR_STEPS[index])),
                device_id_type=MESH,
            )

        edge_copy = pltpu.make_async_remote_copy(
            src_ref=sig_ref.at[:, pl.ds(0, NP)],
            dst_ref=edge_ref,
            send_sem=edge_send,
            recv_sem=edge_recv,
            device_id=(before, pr),
            device_id_type=MESH,
        )
        for index in range(PAIR - 1):
            msg_copy(index, pr).start()

        @pl.when(tm > 0)
        def send_edge():
            edge_copy.start()


    with jax.named_scope("hot"):
        for group in range(HOPS // 2):
            rows_ref[2 * group : 2 * group + 2, :] = sig_ref[:, 128 * group : 128 * (group + 1)]

        channel = lax.broadcasted_iota(jnp.int32, (NP, WIDTH), 0)

        def build_hot(chunk, carry):
            start = pl.multiple_of(chunk * WIDTH, WIDTH)
            for side in range(2):
                index = pc_ref[side : side + 1, pl.ds(start, WIDTH)]
                index = (index >> 1) + (index & 1) * (NP // 2)
                hot_ref[chunk, side] = jnp.where(channel == index, 1.0, 0.0).astype(BF16)
            return carry

        loads[2].wait()
        lax.fori_loop(0, CHUNKS, build_hot, 0)
        loads[3].wait()
        loads[4].wait()

    with jax.named_scope("exchange_wait"):
        others = msg_ref.at[pl.ds(0, PAIR - 1)]
        arrived = pltpu.make_async_remote_copy(
            src_ref=others,
            dst_ref=others,
            send_sem=msg_send,
            recv_sem=msg_recv,
            device_id=(tm, pair_peer(pr, PAIR_STEPS[0])),
            device_id_type=MESH,
        )
        rows_ref[HOPS : HOPS + 8, :] = jnp.zeros((8, 128), F32)

        @pl.when(tm < TM - 1)
        def take_edge():
            edge_copy.wait_recv()
            rows_ref[HOPS : HOPS + 2, :] = edge_ref[:, :128]
            rows_ref[HOPS + 2 : HOPS + 4, :] = edge_ref[:, 128:]

        arrived.wait_recv()
        arrived.wait_send()

        @pl.when(tm > 0)
        def edge_left():
            edge_copy.wait_send()


def main_kernel(
    rows_ref, msg_ref, hot_ref, tab_ref, win_ref, out_ref,
    grid_ref, spec_ref, part_ref, recv_ref,
    part_send, part_recv, done_send, done_recv,
):
    tm = lax.axis_index("tm")
    pr = lax.axis_index("pair")
    with jax.named_scope("greet"):
        barrier = pltpu.get_barrier_semaphore()
        peers = [tm_peer(tm, step) for step in TM_STEPS]
        for peer in peers:
            pl.semaphore_signal(barrier, inc=1, device_id=(peer, pr), device_id_type=MESH)

    with jax.named_scope("frames"):
        messages = msg_ref[...].reshape(Q, 128)
        column = lax.broadcasted_iota(jnp.int32, (Q, 128), 1).astype(F32)

        def samples(part, half, ahead):
            return rows_ref[pl.ds(2 * half + part + 4 * ahead, Q, stride=4), :]

        for u in range(4):
            start = messages[:, u : u + 1]
            cosine = messages[:, 4 + u : 5 + u]
            sine = messages[:, 8 + u : 9 + u]
            halves = []
            for half in range(2):
                lanes = slice(128 * half, 128 * half + 128)
                weight = win_ref[0:1, lanes] + cosine * win_ref[1:2, lanes] + sine * win_ref[2:3, lanes]
                here = column + 128.0 * half >= start
                halves.append(
                    [jnp.where(here, samples(part, half, 0), samples(part, half, 1)) * weight for part in range(2)]
                )
            for sign in range(2):
                for part in range(2):
                    left, right = halves[0][part], halves[1][part]
                    high, low = high_low(left - right if sign else left + right)
                    grid_ref[sign, 0, u * Q : (u + 1) * Q, 128 * part : 128 * (part + 1)] = high
                    grid_ref[sign, 1, u * Q : (u + 1) * Q, 128 * part : 128 * (part + 1)] = low

    with jax.named_scope("spectra"):
        for odd in range(2):
            high, low = grid_ref[odd, 0], grid_ref[odd, 1]
            result = dot(high, tab_ref[2 * odd]) + dot(low, tab_ref[2 * odd]) + dot(high, tab_ref[2 * odd + 1])
            high, low = high_low(result)
            for u in range(4):
                for block in range(BLOCKS):
                    source = slice(u * Q + 16 * block, u * Q + 16 * block + 16)
                    for part in range(2):
                        target = slice(block * 128 + part * 64 + 16 * u, block * 128 + part * 64 + 16 * u + 16)
                        lanes = slice(128 * part, 128 * part + 128)
                        spec_ref[target, 128 * odd : 128 * odd + 128] = high[source, lanes]
                        spec_ref[target, 256 + 128 * odd : 384 + 128 * odd] = low[source, lanes]

    def part_copy(group, index):
        return pltpu.make_async_remote_copy(
            src_ref=part_ref.at[group, peers[index]],
            dst_ref=recv_ref.at[group, index],
            send_sem=part_send,
            recv_sem=part_recv.at[group],
            device_id=(peers[index], pr),
            device_id_type=MESH,
        )

    def slice_of(group, owner):
        rows = pl.ds(pl.multiple_of(8 * (owner % 8), 8), 8)
        return rows, pl.ds(pl.multiple_of(WIDTH * (2 * group + owner // 8), WIDTH), WIDTH)

    def done_copy(group, index, owner):
        rows, lanes = slice_of(group, owner)
        return pltpu.make_async_remote_copy(
            src_ref=out_ref.at[rows, lanes],
            dst_ref=out_ref.at[rows, lanes],
            send_sem=done_send,
            recv_sem=done_recv,
            device_id=(peers[index], pr),
            device_id_type=MESH,
        )

    with jax.named_scope("main"):
        def pick(chunk):
            return [
                dot(spec_ref[:, :NP], hot_ref[chunk, side]) + dot(spec_ref[:, NP:], hot_ref[chunk, side])
                for side in range(2)
            ]

        def power_of(first, second):
            power = None
            for block in range(BLOCKS):
                base = block * 2 * Q
                first_re, first_im = first[base : base + Q], first[base + Q : base + 2 * Q]
                second_re, second_im = second[base : base + Q], second[base + Q : base + 2 * Q]
                re_high, re_low = high_low(first_re * second_re + first_im * second_im)
                im_high, im_low = high_low(first_im * second_re - first_re * second_im)
                stacked = jnp.concatenate([re_high, im_high, re_low, im_low], axis=0)
                both = dot(tab_ref[4], stacked)
                cyclic = both[: 2 * Q] + both[2 * Q :]
                square = cyclic * cyclic
                square = square[:Q] + square[Q:]
                power = square if power is None else power + square
            return power

        for chunk in range(CHUNKS):
            power = power_of(*pick(chunk))
            group, side = chunk // 2, chunk % 2
            for row in range(8):
                part_ref[group, 8 * side + row] = power[8 * row : 8 * row + 8]
            if side:
                if group == 0:
                    pl.semaphore_wait(barrier, TM - 1)
                for index in range(TM - 1):
                    part_copy(group, index).start()

    def all_of(target, send_sem, recv_sem):
        return pltpu.make_async_remote_copy(
            src_ref=target,
            dst_ref=target,
            send_sem=send_sem,
            recv_sem=recv_sem,
            device_id=(peers[0], pr),
            device_id_type=MESH,
        )

    for group in range(GROUPS):
        with jax.named_scope("absorb"):
            all_of(recv_ref.at[group], part_send, part_recv.at[group]).wait_recv()
            total = part_ref[group, tm]
            for index in range(TM - 1):
                total = total + recv_ref[group, index]
            rows, lanes = slice_of(group, tm)
            out_ref[rows, lanes] = total * (1.0 / Q)
            for index in range(TM - 1):
                done_copy(group, index, tm).start()

    with jax.named_scope("gather_wait"):
        all_done = all_of(recv_ref, done_send, done_recv)
        all_done.wait_recv()

    with jax.named_scope("drain"):
        all_of(recv_ref, part_send, done_recv).wait_send()
        all_done.wait_send()


def in_hbm(array):
    return pltpu.with_memory_space_constraint(array, pltpu.HBM)


def in_vmem(array):
    return pltpu.with_memory_space_constraint(array, pltpu.VMEM)


def shards(signal, hop_offsets, pair_channels):
    vmem = pl.BlockSpec(memory_space=pltpu.VMEM)
    hbm = pl.BlockSpec(memory_space=pltpu.HBM)
    passed = (
        ((HOPS + 8, 128), F32),
        ((PAIR, 8, 128), F32),
        ((CHUNKS, 2, NP, WIDTH), BF16),
        ((5, NP, NP), BF16),
        ((8, NP), F32),
    )
    staged = pl.pallas_call(
        exchange_kernel,
        out_shape=[pltpu.VMEM(*shape) for shape in passed],
        in_specs=[hbm] * 5,
        out_specs=[vmem] * 5,
        scratch_shapes=[
            pltpu.VMEM((2, HOPS * Q), F32),
            pltpu.VMEM((1, HOPS // PAIR), jnp.int32),
            pltpu.VMEM((2, PAIRS), jnp.int32),
            pltpu.VMEM((2, NP), F32),
            pltpu.SemaphoreType.DMA((5,)),
            pltpu.SemaphoreType.DMA,
            pltpu.SemaphoreType.DMA,
            pltpu.SemaphoreType.DMA,
            pltpu.SemaphoreType.DMA,
        ],
        compiler_params=pltpu.CompilerParams(
            collective_id=0, has_side_effects=True, vmem_limit_bytes=16 * 1024 * 1024
        ),
    )(
        in_hbm(signal),
        in_hbm(hop_offsets.reshape(1, HOPS // PAIR)),
        in_hbm(pair_channels),
        in_hbm(jnp.asarray(window_rows())),
        in_hbm(jnp.asarray(tables())),
    )
    return pl.pallas_call(
        main_kernel,
        out_shape=jax.ShapeDtypeStruct((Q, PAIRS), F32),
        in_specs=[vmem] * 5,
        out_specs=vmem,
        scratch_shapes=[
            pltpu.VMEM((2, 2, HOPS, NP), BF16),
            pltpu.VMEM((2 * HOPS, 2 * NP), BF16),
            pltpu.VMEM((GROUPS, TM, 8, WIDTH), F32),
            pltpu.VMEM((GROUPS, TM - 1, 8, WIDTH), F32),
            pltpu.SemaphoreType.DMA,
            pltpu.SemaphoreType.DMA((GROUPS,)),
            pltpu.SemaphoreType.DMA,
            pltpu.SemaphoreType.DMA,
        ],
        compiler_params=pltpu.CompilerParams(
            collective_id=1, has_side_effects=True, vmem_limit_bytes=32 * 1024 * 1024
        ),
    )(*(in_vmem(array) for array in staged))


def solution(mesh):
    return jax.shard_map(
        shards,
        mesh=mesh,
        in_specs=(P(None, "tm"), P(("tm", "pair")), P(None, "pair")),
        out_specs=P(None, "pair"),
        check_vma=False,
    )
```

time: 34 us -> 28.2 us (0.83)
  Pallas kernels: 33.1 us -> 27.1 us
    pallas_call x1 -> x2, Pallas kernels: 33.1 us -> 27.1 us  [the longest x1 19.8 us: shards(): pl.pallas_call(main_kernel, out_shape=jax.ShapeDtypeStruct((Q, PAIRS), F3...]
where the time goes in v3:
time: 28.2 us; the launch traced here: 27.9 us
  Pallas kernels  27.1 us (96%)
  local copies, waits for them, and re-layouts  0.8 us (3%)
    pallas_call x1, Pallas kernels, shards(): pl.pallas_call(main_kernel, out_shape=jax.ShapeDtypeStruct((Q, PAIRS), F3...  19.8 us
    pallas_call x1, Pallas kernels, shards(): pl.pallas_call(exchange_kernel, out_shape=[pltpu.VMEM(*shape) for shape i...  7.27 us
    unnamed x1, local copies, waits for them, and re-layouts  0.8 us

profile of v3, /device:TPU:1, one launch (start us, length us, event | category | flops | bytes accessed | tf_op | source)
XLA Modules:
  0.0 27.9 jit_solution(16833538240785694864)
XLA Ops:
  0.0 7.3 %shard_map.55 = (f32[264,128]{1,0:T(8,128)S(1)}, f32[8,8,128]{2,1,0:T(8,128)S(1)}, bf16[8,2,256,256]{3,2,1,0:T(8,128)(2,1)S(1)}, bf16[5,256,256]{2,1,0:T(8,128)(2,1)S(1)}, f32[8,256]{1,0:T(8,128)S(1)}) custom-call(f32[2,16384]{1,0:T(2,128)} %sig_hbm.1, s32[1,32]{1,0:T(1,128)} %bitcast.1, s32[2,2048]{1,0:T(2,128)} %pc_hbm.1, f32[8,256]{1,0:T(8,128)} %constant.4.clone.win_hbm, ...), custom_call_target="tpu_custom_call" | custom-call | tf_op jit(solution)/shard_map/pallas_call | solution.py:384
  7.3 19.8 %shard_map.56 = f32[64,2048]{1,0:T(8,128)S(1)} custom-call(f32[264,128]{1,0:T(8,128)S(1)} %get-tuple-element.10.rows_ref, f32[8,8,128]{2,1,0:T(8,128)S(1)} %get-tuple-element.11.msg_ref, bf16[8,2,256,256]{3,2,1,0:T(8,128)(2,1)S(1)} %get-tuple-element.12.hot_ref, bf16[5,256,256]{2,1,0:T(8,128)(2,1)S(1)} %get-tuple-element.13.tab_ref, ...), custom_call_target="tpu_custom_call" | custom-call | tf_op jit(solution)/shard_map/pallas_call | solution.py:410
  27.1 0.8 %copy.7 = f32[64,2048]{1,0:T(8,128)} copy(f32[64,2048]{1,0:T(8,128)S(1)} %shard_map.56) | data formatting | bytes 1048576

commit v4 on v3

--- a/solution.py
+++ b/solution.py
@@ -15,7 +15,9 @@
 PAIRS = 2048
 WIDTH = 256
 CHUNKS = PAIRS // WIDTH
-GROUPS = CHUNKS // 2
+STAGED = ((0, 2), (2, 4), (4, 6), (6, 8))
+STAGED_CHUNKS = STAGED[-1][1]
+ORDER = tuple((name, group) for name in ("first", "second") for group in range(len(STAGED)))
 BLOCKS = HOPS // Q
 MESH = pl.DeviceIdType.MESH
 F32 = jnp.float32
@@ -93,27 +95,43 @@
     return ((pr // 2 + sign * dy) % 4) * 2 + (pr % 2 + dc) % 2
 
 
-def exchange_kernel(
-    sig_hbm, off_hbm, pc_hbm, win_hbm, tab_hbm,
-    rows_ref, msg_ref, hot_ref, tab_ref, win_ref,
-    sig_ref, off_ref, pc_ref, edge_ref,
-    load_sem, edge_send, edge_recv, msg_send, msg_recv,
+def kernel(
+    sig_hbm, off_hbm, pc_hbm, win_hbm, tab_hbm, out_ref,
+    sig_ref, off_ref, pc_ref, win_ref, tab_ref, rows_ref, edge_ref, msg_ref, hot_ref,
+    grid_ref, spec_ref, pair_ref, part_ref, first_ref, mid_ref, done_ref,
+    load_sem, ready_sem, edge_send, edge_recv, msg_send, msg_recv,
+    stage_send, stage_recv,
 ):
     tm = lax.axis_index("tm")
     pr = lax.axis_index("pair")
     before = (tm + TM - 1) % TM
     after = (tm + 1) % TM
+    peers = [tm_peer(tm, step) for step in TM_STEPS]
+    in_row = [peer for peer, (dz, dx) in zip(peers, TM_STEPS) if dz == 0]
+    tm_row, tm_column = tm // 4, tm % 4
+    far_before = (tm_column == 0) & (tm_row > 0)
+    far_after = (tm_column == 3) & (tm_row < 3)
+
+    def signal(semaphore, peer):
+        pl.semaphore_signal(semaphore, inc=1, device_id=(peer, pr), device_id_type=MESH)
+
+    def signal_column(semaphore, first, last):
+        lax.fori_loop(first, last, lambda z, carry: signal(semaphore, 4 * z + tm_column), None)
+
+    def signal_row(semaphore, first, last):
+        lax.fori_loop(first, last, lambda x, carry: signal(semaphore, 4 * tm_row + x), None)
 
     with jax.named_scope("load_greet"):
         barrier = pltpu.get_barrier_semaphore()
-        for near, peer in ((tm > 0, before), (tm < TM - 1, after)):
-
-            @pl.when(near)
-            def greet():
-                pl.semaphore_signal(barrier, inc=1, device_id=(peer, pr), device_id_type=MESH)
-
         for step in PAIR_STEPS:
             pl.semaphore_signal(barrier, inc=1, device_id=(tm, pair_peer(pr, step)), device_id_type=MESH)
+        signal_column(barrier, tm_row + 1, jnp.int32(4))
+        signal_row(barrier, tm_column + 1, jnp.int32(4))
+
+        @pl.when(far_after)
+        def greet():
+            signal(barrier, after)
+
         loads = [
             pltpu.make_async_copy(source, target, load_sem.at[index])
             for index, (source, target) in enumerate(
@@ -146,8 +164,7 @@
         loads[1].wait()
 
     with jax.named_scope("barrier"):
-        ends = jnp.where((tm == 0) | (tm == TM - 1), 1, 2)
-        pl.semaphore_wait(barrier, PAIR - 1 + ends)
+        pl.semaphore_wait(barrier, PAIR - 1 + tm_row + tm_column + jnp.where(far_before, 1, 0))
 
     with jax.named_scope("exchange_start"):
         def msg_copy(index, slot):
@@ -175,6 +192,8 @@
         def send_edge():
             edge_copy.start()
 
+        signal_column(ready_sem, jnp.int32(0), tm_row)
+        signal_row(ready_sem, jnp.int32(0), tm_column)
 
     with jax.named_scope("hot"):
         for group in range(HOPS // 2):
@@ -194,6 +213,11 @@
         lax.fori_loop(0, CHUNKS, build_hot, 0)
         loads[3].wait()
         loads[4].wait()
+
+    with jax.named_scope("ready"):
+        @pl.when(tm < TM - 1)
+        def wait_ready():
+            pl.semaphore_wait(ready_sem, 6 - tm_row - tm_column)
 
     with jax.named_scope("exchange_wait"):
         others = msg_ref.at[pl.ds(0, PAIR - 1)]
@@ -219,20 +243,6 @@
         @pl.when(tm > 0)
         def edge_left():
             edge_copy.wait_send()
-
-
-def main_kernel(
-    rows_ref, msg_ref, hot_ref, tab_ref, win_ref, out_ref,
-    grid_ref, spec_ref, part_ref, recv_ref,
-    part_send, part_recv, done_send, done_recv,
-):
-    tm = lax.axis_index("tm")
-    pr = lax.axis_index("pair")
-    with jax.named_scope("greet"):
-        barrier = pltpu.get_barrier_semaphore()
-        peers = [tm_peer(tm, step) for step in TM_STEPS]
-        for peer in peers:
-            pl.semaphore_signal(barrier, inc=1, device_id=(peer, pr), device_id_type=MESH)
 
     with jax.named_scope("frames"):
         messages = msg_ref[...].reshape(Q, 128)
@@ -274,44 +284,61 @@
                         spec_ref[target, 128 * odd : 128 * odd + 128] = high[source, lanes]
                         spec_ref[target, 256 + 128 * odd : 384 + 128 * odd] = low[source, lanes]
 
-    def part_copy(group, index):
+    def stage_copy(group, chunk, stage, step):
+        even = chunk % 2 == 0
+        mine, other = (tm_column, tm_row) if even else (tm_row, tm_column)
+        if even == (stage != 1):
+            peer = 4 * tm_row + (tm_column + step) % 4
+        else:
+            peer = 4 * ((tm_row + step) % 4) + tm_column
+        if stage == 0:
+            source, target = part_ref.at[chunk, (mine + step) % 4], first_ref.at[chunk, step - 1]
+        elif stage == 1:
+            source = target = mid_ref.at[chunk, other]
+        else:
+            source = target = done_ref.at[chunk, mine]
         return pltpu.make_async_remote_copy(
-            src_ref=part_ref.at[group, peers[index]],
-            dst_ref=recv_ref.at[group, index],
-            send_sem=part_send,
-            recv_sem=part_recv.at[group],
-            device_id=(peers[index], pr),
+            src_ref=source,
+            dst_ref=target,
+            send_sem=stage_send.at[stage],
+            recv_sem=stage_recv.at[3 * group + stage],
+            device_id=(peer, pr),
             device_id_type=MESH,
         )
 
-    def slice_of(group, owner):
-        rows = pl.ds(pl.multiple_of(8 * (owner % 8), 8), 8)
-        return rows, pl.ds(pl.multiple_of(WIDTH * (2 * group + owner // 8), WIDTH), WIDTH)
-
-    def done_copy(group, index, owner):
-        rows, lanes = slice_of(group, owner)
+    def send_stage(group, stage):
+        for step in (2, 1, 3):
+            for chunk in range(*STAGED[group]):
+                stage_copy(group, chunk, stage, step).start()
+
+    def all_of(target, send_sem, recv_sem):
         return pltpu.make_async_remote_copy(
-            src_ref=out_ref.at[rows, lanes],
-            dst_ref=out_ref.at[rows, lanes],
-            send_sem=done_send,
-            recv_sem=done_recv,
-            device_id=(peers[index], pr),
+            src_ref=target,
+            dst_ref=target,
+            send_sem=send_sem,
+            recv_sem=recv_sem,
+            device_id=(peers[0], pr),
             device_id_type=MESH,
         )
 
+    def wait_stage(group, stage):
+        first, last = STAGED[group]
+        target = first_ref.at[pl.ds(first, last - first)]
+        all_of(target, stage_send.at[stage], stage_recv.at[3 * group + stage]).wait_recv()
+
     with jax.named_scope("main"):
         def pick(chunk):
-            return [
-                dot(spec_ref[:, :NP], hot_ref[chunk, side]) + dot(spec_ref[:, NP:], hot_ref[chunk, side])
-                for side in range(2)
-            ]
-
-        def power_of(first, second):
+            for side in range(2):
+                pair_ref[chunk % 2, side] = dot(spec_ref[:, :NP], hot_ref[chunk, side]) + dot(
+                    spec_ref[:, NP:], hot_ref[chunk, side]
+                )
+
+        def power_of(slot):
             power = None
             for block in range(BLOCKS):
                 base = block * 2 * Q
-                first_re, first_im = first[base : base + Q], first[base + Q : base + 2 * Q]
-                second_re, second_im = second[base : base + Q], second[base + Q : base + 2 * Q]
+                first_re, first_im = (pair_ref[slot, 0, base + Q * part : base + Q * part + Q] for part in range(2))
+                second_re, second_im = (pair_ref[slot, 1, base + Q * part : base + Q * part + Q] for part in range(2))
                 re_high, re_low = high_low(first_re * second_re + first_im * second_im)
                 im_high, im_low = high_low(first_im * second_re - first_re * second_im)
                 stacked = jnp.concatenate([re_high, im_high, re_low, im_low], axis=0)
@@ -322,83 +349,93 @@
                 power = square if power is None else power + square
             return power
 
+        pick(0)
+        staged_ends = [last for first, last in STAGED]
         for chunk in range(CHUNKS):
-            power = power_of(*pick(chunk))
-            group, side = chunk // 2, chunk % 2
-            for row in range(8):
-                part_ref[group, 8 * side + row] = power[8 * row : 8 * row + 8]
-            if side:
-                if group == 0:
-                    pl.semaphore_wait(barrier, TM - 1)
-                for index in range(TM - 1):
-                    part_copy(group, index).start()
-
-    def all_of(target, send_sem, recv_sem):
-        return pltpu.make_async_remote_copy(
-            src_ref=target,
-            dst_ref=target,
-            send_sem=send_sem,
-            recv_sem=recv_sem,
-            device_id=(peers[0], pr),
-            device_id_type=MESH,
-        )
-
-    for group in range(GROUPS):
-        with jax.named_scope("absorb"):
-            all_of(recv_ref.at[group], part_send, part_recv.at[group]).wait_recv()
-            total = part_ref[group, tm]
-            for index in range(TM - 1):
-                total = total + recv_ref[group, index]
-            rows, lanes = slice_of(group, tm)
-            out_ref[rows, lanes] = total * (1.0 / Q)
-            for index in range(TM - 1):
-                done_copy(group, index, tm).start()
-
-    with jax.named_scope("gather_wait"):
-        all_done = all_of(recv_ref, done_send, done_recv)
-        all_done.wait_recv()
-
+            if chunk + 1 < CHUNKS:
+                pick(chunk + 1)
+            power = power_of(chunk % 2)
+            for tile in range(TM):
+                rows, lanes = 8 * (tile % 8), 128 * (tile // 8)
+                part_ref[chunk, tile // 4, tile % 4] = power[rows : rows + 8, lanes : lanes + 128]
+            if chunk + 1 in staged_ends:
+                send_stage(staged_ends.index(chunk + 1), 0)
+
+    def sum_first(group):
+        wait_stage(group, 0)
+        for chunk in range(*STAGED[group]):
+            mine, other = (tm_column, tm_row) if chunk % 2 == 0 else (tm_row, tm_column)
+            total = part_ref[chunk, mine]
+            for step in range(3):
+                total = total + first_ref[chunk, step]
+            mid_ref[chunk, other] = total
+        send_stage(group, 1)
+
+    def sum_second(group):
+        wait_stage(group, 1)
+        for chunk in range(*STAGED[group]):
+            mine = tm_column if chunk % 2 == 0 else tm_row
+            total = (mid_ref[chunk, 0] + mid_ref[chunk, 1]) + (mid_ref[chunk, 2] + mid_ref[chunk, 3])
+            done_ref[chunk, mine] = total * (1.0 / Q)
+        send_stage(group, 2)
+
+    def put_out(chunks):
+        for chunk in range(*chunks):
+            for tile in range(TM):
+                rows, lanes = 8 * (tile % 8), WIDTH * chunk + 128 * (tile // 8)
+                out_ref[rows : rows + 8, lanes : lanes + 128] = done_ref[chunk, tile // 4, tile % 4]
+
+    actions = {"first": sum_first, "second": sum_second}
+    for name, group in ORDER:
+        with jax.named_scope(f"{name}{group}"):
+            actions[name](group)
+    for group in range(len(STAGED)):
+        with jax.named_scope(f"third{group}"):
+            wait_stage(group, 2)
+            put_out(STAGED[group])
     with jax.named_scope("drain"):
-        all_of(recv_ref, part_send, done_recv).wait_send()
-        all_done.wait_send()
+        for stage in range(3):
+            all_of(first_ref, stage_send.at[stage], stage_recv.at[stage]).wait_send()
 
 
 def in_hbm(array):
     return pltpu.with_memory_space_constraint(array, pltpu.HBM)
 
 
-def in_vmem(array):
-    return pltpu.with_memory_space_constraint(array, pltpu.VMEM)
-
-
 def shards(signal, hop_offsets, pair_channels):
-    vmem = pl.BlockSpec(memory_space=pltpu.VMEM)
-    hbm = pl.BlockSpec(memory_space=pltpu.HBM)
-    passed = (
-        ((HOPS + 8, 128), F32),
-        ((PAIR, 8, 128), F32),
-        ((CHUNKS, 2, NP, WIDTH), BF16),
-        ((5, NP, NP), BF16),
-        ((8, NP), F32),
-    )
-    staged = pl.pallas_call(
-        exchange_kernel,
-        out_shape=[pltpu.VMEM(*shape) for shape in passed],
-        in_specs=[hbm] * 5,
-        out_specs=[vmem] * 5,
+    return pl.pallas_call(
+        kernel,
+        out_shape=jax.ShapeDtypeStruct((Q, PAIRS), F32),
+        in_specs=[pl.BlockSpec(memory_space=pltpu.HBM)] * 5,
+        out_specs=pl.BlockSpec(memory_space=pltpu.VMEM),
         scratch_shapes=[
             pltpu.VMEM((2, HOPS * Q), F32),
             pltpu.VMEM((1, HOPS // PAIR), jnp.int32),
             pltpu.VMEM((2, PAIRS), jnp.int32),
+            pltpu.VMEM((8, NP), F32),
+            pltpu.VMEM((5, NP, NP), BF16),
+            pltpu.VMEM((HOPS + 8, 128), F32),
             pltpu.VMEM((2, NP), F32),
+            pltpu.VMEM((PAIR, 8, 128), F32),
+            pltpu.VMEM((CHUNKS, 2, NP, WIDTH), BF16),
+            pltpu.VMEM((2, 2, HOPS, NP), BF16),
+            pltpu.VMEM((2 * HOPS, 2 * NP), BF16),
+            pltpu.VMEM((2, 2, 2 * HOPS, WIDTH), F32),
+            pltpu.VMEM((CHUNKS, 4, 4, 8, 128), F32),
+            pltpu.VMEM((STAGED_CHUNKS, 3, 4, 8, 128), F32),
+            pltpu.VMEM((STAGED_CHUNKS, 4, 4, 8, 128), F32),
+            pltpu.VMEM((CHUNKS, 4, 4, 8, 128), F32),
             pltpu.SemaphoreType.DMA((5,)),
+            pltpu.SemaphoreType.REGULAR,
             pltpu.SemaphoreType.DMA,
             pltpu.SemaphoreType.DMA,
             pltpu.SemaphoreType.DMA,
             pltpu.SemaphoreType.DMA,
+            pltpu.SemaphoreType.DMA((3,)),
+            pltpu.SemaphoreType.DMA((3 * len(STAGED),)),
         ],
         compiler_params=pltpu.CompilerParams(
-            collective_id=0, has_side_effects=True, vmem_limit_bytes=16 * 1024 * 1024
+            collective_id=0, has_side_effects=True, vmem_limit_bytes=48 * 1024 * 1024
         ),
     )(
         in_hbm(signal),
@@ -407,25 +444,6 @@
         in_hbm(jnp.asarray(window_rows())),
         in_hbm(jnp.asarray(tables())),
     )
-    return pl.pallas_call(
-        main_kernel,
-        out_shape=jax.ShapeDtypeStruct((Q, PAIRS), F32),
-        in_specs=[vmem] * 5,
-        out_specs=vmem,
-        scratch_shapes=[
-            pltpu.VMEM((2, 2, HOPS, NP), BF16),
-            pltpu.VMEM((2 * HOPS, 2 * NP), BF16),
-            pltpu.VMEM((GROUPS, TM, 8, WIDTH), F32),
-            pltpu.VMEM((GROUPS, TM - 1, 8, WIDTH), F32),
-            pltpu.SemaphoreType.DMA,
-            pltpu.SemaphoreType.DMA((GROUPS,)),
-            pltpu.SemaphoreType.DMA,
-            pltpu.SemaphoreType.DMA,
-        ],
-        compiler_params=pltpu.CompilerParams(
-            collective_id=1, has_side_effects=True, vmem_limit_bytes=32 * 1024 * 1024
-        ),
-    )(*(in_vmem(array) for array in staged))
 
 
 def solution(mesh):

time: 28.2 us -> 26.7 us (0.947)
  the two profiles are of different devices: /device:TPU:1 before, /device:TPU:0 now
where the time goes in v4:
time: 26.7 us; the launch traced here: 26.6 us
  Pallas kernels  25.8 us (97%)
  local copies, waits for them, and re-layouts  0.8 us (3%)
    pallas_call x1, Pallas kernels, shards(): pl.pallas_call(kernel, out_shape=jax.ShapeDtypeStruct((Q, PAIRS), F32), i...  25.8 us
    unnamed x1, local copies, waits for them, and re-layouts  0.8 us

profile of v4, /device:TPU:0, one launch (start us, length us, event | category | flops | bytes accessed | tf_op | source)
XLA Modules:
  0.0 26.6 jit_solution(3998813934409921486)
XLA Ops:
  0.0 25.8 %shard_map.55 = f32[64,2048]{1,0:T(8,128)S(1)} custom-call(f32[2,16384]{1,0:T(2,128)} %sig_hbm.1, s32[1,32]{1,0:T(1,128)} %bitcast.1, s32[2,2048]{1,0:T(2,128)} %pc_hbm.1, f32[8,256]{1,0:T(8,128)} %constant.4.clone.win_hbm, bf16[5,256,256]{2,1,0:T(8,128)(2,1)} %constant.5.clone.tab_hbm), custom_call_target="tpu_custom_call" | custom-call | tf_op jit(solution)/shard_map/pallas_call | solution.py:406
  25.8 0.8 %copy.7 = f32[64,2048]{1,0:T(8,128)} copy(f32[64,2048]{1,0:T(8,128)S(1)} %shard_map.55) | data formatting | bytes 1048576
